TPU v7x, 128 devices: a whole 4x4x4 slice. The times are simulated.
128 devices in a mesh: rep: 8 (over y, z_lo), tp: 16 (over x, z_hi, core).
Axes of the slice: x: 4, y: 4, z: 4 (z_hi: 2, z_lo: 2; z = z_hi * 2 + z_lo), core: 2. Of those that a mesh axis runs over, the one named last changes fastest.
Arguments:
- deltas: bfloat16 [8, 3, 4096, 8192], P('rep', None, 'tp'), may hold values from -2600 to 2600
- staleness: int32 [8], P('rep'), may hold values from 0 to 2
Outputs:
- update: bfloat16 [4096, 8192], P('tp')
All inputs are finite; a program needn't handle non-finite values.
Results may differ from a plain program's by a relative error of at most 0.028.
Values may be sent and summed in bfloat16 or wider, within the bound.
No kernel may reach another device: no remote copies, remote signals or barrier semaphores. Data moves between devices by JAX's collectives and lax.ppermute only.
A program may use at most 128 MiB of HBM per device.

v0:
```python
import jax
import jax.numpy as jnp
from jax import lax
from jax.sharding import PartitionSpec as P

TILE = 512
NS_ITERS = 5


damping = 0.001


def in_blocks(shard, dim, length):
    shape = shard.shape
    pieces = shard.reshape(*shape[:dim], length, shape[dim] // length, *shape[dim + 1 :])
    return jnp.moveaxis(pieces, dim, 0)


def cut_rows(length, count):
    unit = 8 if length >= 8 * count else 1
    return [length // unit * k // count * unit for k in range(1, count)]


def in_order(pieces, dim):
    pieces = jnp.moveaxis(pieces, 0, dim)
    shape = pieces.shape
    return pieces.reshape(*shape[:dim], shape[dim] * shape[dim + 1], *shape[dim + 2 :])


def cut_exchange(shard, axis, pieces, split_dim, concat_dim):
    blocks = in_blocks(shard, split_dim, lax.axis_size(axis))
    split_at = max(range(1, max(2, blocks.ndim - 1)), key=lambda d: blocks.shape[d])
    done = []
    for share in jnp.split(blocks, cut_rows(blocks.shape[split_at], pieces), axis=split_at):
        if share.size:
            done.append(lax.all_to_all(share, axis, split_axis=0, concat_axis=0, tiled=True))
    return in_order(jnp.concatenate(done, axis=split_at), concat_dim)


def multiply(left_side, right_side):
    return jnp.einsum("xij,xjk->xik", left_side, right_side)


def inverse_roots(stat_stack):
    identity = jnp.eye(TILE, dtype=jnp.float32)
    frob_norm = jnp.sqrt(jnp.sum(stat_stack * stat_stack, axis=(1, 2), keepdims=True))
    current = stat_stack / frob_norm
    iterate = jnp.broadcast_to(identity, stat_stack.shape)
    for step in range(NS_ITERS):
        factor = (5.0 * identity - current) * 0.25
        iterate = multiply(iterate, factor)
        if step + 1 < NS_ITERS:
            square = multiply(factor, factor)
            fourth = multiply(square, square)
            current = multiply(fourth, current)
    return (iterate * frob_norm ** (-0.25)).astype(jnp.bfloat16)


def to_grid(strip_rows, tile):
    return strip_rows.reshape(
        strip_rows.shape[0] // tile, tile, strip_rows.shape[1] // tile, tile
    ).transpose(0, 2, 1, 3)


def to_strip(tile_grid):
    grid_rows, grid_cols, tile, _ = tile_grid.shape
    return tile_grid.transpose(0, 2, 1, 3).reshape(grid_rows * tile, grid_cols * tile)


def precondition(root_grid, mean_tiles):
    half_product = jnp.einsum(
        "abij,abjk->abik", root_grid[:, :, 0], mean_tiles, preferred_element_type=jnp.float32
    ).astype(jnp.bfloat16)
    return jnp.einsum(
        "abij,abjk->abik", half_product, root_grid[:, :, 1], preferred_element_type=jnp.float32
    ).astype(jnp.bfloat16)


def local(deltas, staleness):
    replicas = lax.axis_size("rep")
    picked = lax.dynamic_index_in_dim(deltas[0], staleness[0], 0, keepdims=False)
    column_strip = lax.all_to_all(picked, "tp", split_axis=1, concat_axis=0, tiled=True)
    grid_rows = column_strip.shape[0] // TILE
    grid_cols = column_strip.shape[1] // TILE
    own_rows = grid_rows // replicas
    received = cut_exchange(column_strip[None], "rep", 2, 1, 0)
    replica_grid = received.reshape(replicas, own_rows, TILE, grid_cols, TILE).transpose(
        0, 1, 3, 2, 4
    )
    left_gram = jnp.einsum(
        "rabik,rabjk->abij", replica_grid, replica_grid, preferred_element_type=jnp.float32
    )
    right_gram = jnp.einsum(
        "rabki,rabkj->abij", replica_grid, replica_grid, preferred_element_type=jnp.float32
    )
    gram_sums = jnp.stack([left_gram, right_gram], axis=2).reshape(
        own_rows * grid_cols * 2, TILE, TILE
    )
    strip_sum = jnp.sum(received.astype(jnp.float32), axis=0)
    mean_part = (strip_sum / replicas).astype(jnp.bfloat16)
    identity = jnp.eye(TILE, dtype=jnp.float32)
    root_stack = inverse_roots(gram_sums / (replicas * TILE) + damping * identity)
    local_tiles = precondition(
        root_stack.reshape(own_rows, grid_cols, 2, TILE, TILE), to_grid(mean_part, TILE)
    )
    gathered = lax.all_gather(to_strip(local_tiles), "rep", axis=0, tiled=True)
    return lax.all_to_all(gathered, "tp", split_axis=0, concat_axis=1, tiled=True)


def solution(mesh):
    return jax.shard_map(
        local,
        mesh=mesh,
        in_specs=(P("rep", None, "tp", None), P("rep")),
        out_specs=P("tp", None),
        check_vma=False,
    )
```

profile of v0, /device:TPU:1, one launch (start us, length us, event | category | flops | bytes accessed | tf_op | source)
XLA Modules:
  0.0 368.4 jit_solution(15964659159296157867)
XLA Ops:
  7.2 4.6 %constant_dynamic-slice_fusion = bf16[1,1,256,8192]{3,2,1,0:T(8,128)(2,1)} fusion(bf16[1,3,256,8192]{3,2,1,0:T(8,128)(2,1)} %param.2, s32[]{:T(128)S(6)} %select_n.4), kind=kLoop, calls=%fused_computation.59 | loop fusion | bytes 8388612 | tf_op jit(solution)/shard_map/jit(dynamic_index_in_dim)/dynamic_slice | solution.py:81
  11.8 6.4 %copy.23 = bf16[1,1,256,8192]{2,3,1,0:T(8,128)(2,1)} copy(bf16[1,1,256,8192]{3,2,1,0:T(8,128)(2,1)} %constant_dynamic-slice_fusion) | data formatting | bytes 8388608
  18.2 59.7 %all_to_all.45 = bf16[256,16,512]{0,2,1:T(8,128)(2,1)} all-to-all(bf16[256,16,512]{0,2,1:T(8,128)(2,1)} %bitcast.67), channel_id=1, replica_groups=mesh['rep'=8,'tp'=16] {'tp'}, dimensions={1} | all-to-all | bytes 8388608 | tf_op jit(solution)/shard_map/all_to_all | solution.py:82
  77.9 6.4 %copy.15 = bf16[16,256,512]{2,1,0:T(8,128)(2,1)} copy(bf16[16,256,512]{1,2,0:T(8,128)(2,1)} %bitcast.68) | data formatting | bytes 8388608 | tf_op jit(solution)/shard_map/all_to_all | solution.py:82
  84.3 3.8 %slice_bitcast_fusion.1 = (bf16[8,1,256,512]{3,2,1,0:T(8,128)(2,1)}, bf16[8,1,256,512]{3,2,1,0:T(8,128)(2,1)S(1)}) fusion(bf16[8,1,512,512]{3,2,0,1:T(8,128)(2,1)} %bitcast.66), kind=kLoop, calls=%fused_computation.3 | loop fusion | bytes 8388608 | tf_op jit(solution)/shard_map/split | solution.py:34
  88.2 29.5 %all_to_all.46 = bf16[8,1,256,512]{3,2,1,0:T(8,128)(2,1)S(1)} all-to-all(bf16[8,1,256,512]{3,2,1,0:T(8,128)(2,1)S(1)} %get-tuple-element.6), channel_id=1, replica_groups=mesh['rep'=8,'tp'=16] {'rep'}, dimensions={0} | all-to-all | bytes 4194304 | tf_op jit(solution)/shard_map/all_to_all | solution.py:36
  117.7 4.3 %all-to-all-start.1 = ((bf16[8,1,256,512]{3,2,1,0:T(8,128)(2,1)}), bf16[8,1,256,512]{3,2,1,0:T(8,128)(2,1)}, u32[]{:S(2)}, u32[]{:S(2)}) async-start(bf16[8,1,256,512]{3,2,1,0:T(8,128)(2,1)} %get-tuple-element.5), calls=%async_computation.1 | async-start | bytes 4194304 | tf_op jit(solution)/shard_map/all_to_all | solution.py:36
  122.0 0.0 all-gather.2.cloned.1.call-start
  122.1 0.8 fusion.59
  122.9 1.2 fusion.57
  124.1 26.7 %all-to-all-done.1 = bf16[8,1,256,512]{3,2,1,0:T(8,128)(2,1)} async-done(((bf16[8,1,256,512]{3,2,1,0:T(8,128)(2,1)}), bf16[8,1,256,512]{3,2,1,0:T(8,128)(2,1)}, u32[]{:S(2)}, u32[]{:S(2)}) %all-to-all-start.1) | async-done | bytes 2097184 | tf_op jit(solution)/shard_map/all_to_all | solution.py:36
  150.9 3.3 convert_reduce_fusion
  154.2 4.6 %convolution_bitcast_fusion = f32[1,1,1,512,512]{4,3,2,1,0:T(8,128)S(1)} fusion(bf16[8,1,256,512]{3,2,0,1:T(8,128)(2,1)S(1)} %bitcast.71, bf16[8,1,256,512]{3,2,0,1:T(8,128)(2,1)} %bitcast.5), kind=kOutput, calls=%fused_computation.30 | convolution fusion | flops 2155872256 | bytes 5242880 | tf_op jit(solution)/shard_map/rabki,rabkj->abij/dot_general | solution.py:93
  158.7 0.0 copy-start.4
  158.7 0.0 copy-start
  158.7 5.0 %convolution_bitcast_fusion.1 = f32[1,1,1,512,512]{4,3,2,1,0:T(8,128)S(1)} fusion(bf16[8,1,256,512]{3,2,0,1:T(8,128)(2,1)S(1)} %bitcast.72, bf16[8,1,256,512]{3,2,0,1:T(8,128)(2,1)} %bitcast.5), kind=kOutput, calls=%fused_computation.31 | convolution fusion | flops 2155872256 | bytes 5242880 | tf_op jit(solution)/shard_map/rabik,rabjk->abij/dot_general | solution.py:90
  163.7 0.0 copy-start.6
  163.7 0.0 copy-start.1
  163.7 0.0 copy-done.4
  163.8 0.0 copy-done
  163.8 0.5 multiply_reduce_fusion
  164.2 0.4 copy-done.6
  164.7 0.6 copy-done.1
  165.3 0.0 copy-start.5
  165.3 7.4 %fusion.14 = bf16[2,512,512]{2,1,0:T(8,128)(2,1)} fusion(f32[512,512]{1,0:T(8,128)S(1)} %get-tuple-element.10, f32[1,1,1,512,512]{4,3,2,1,0:T(8,128)} %copy-done.4, f32[1,1,1,512,512]{4,3,2,1,0:T(8,128)} %copy-done.6, f32[2]{0:T(128)S(1)} %get-tuple-element.8, f32[512,512]{1,0:T(8,128)S(1)} %copy-done.1), kind=kOutput, calls=%fused_computation.22 | convolution fusion | flops 1076887552 | bytes 5242888 | tf_op jit(solution)/shard_map/xij,xjk->xik/dot_general | solution.py:41
  172.7 0.0 copy-done.5
  172.7 3.7 fusion.81
  176.4 6.5 %fusion.11 = bf16[2,512,512]{2,1,0:T(8,128)(2,1)} fusion(f32[2,512,512]{2,1,0:T(8,128)} %fusion.81, f32[512,512]{1,0:T(8,128)S(1)} %get-tuple-element.10), kind=kOutput, calls=%fused_computation.20 | convolution fusion | flops 1074790400 | bytes 4194304 | tf_op jit(solution)/shard_map/xij,xjk->xik/dot_general | solution.py:41
  182.9 4.5 %fusion.18 = bf16[2,512,512]{2,1,0:T(8,128)(2,1)} fusion(f32[2,512,512]{2,1,0:T(8,128)} %fusion.81, f32[512,512]{1,0:T(8,128)S(1)} %get-tuple-element.10, bf16[512,512]{1,0:T(8,128)(2,1)} %fusion.59, f32[1,1,1,512,512]{4,3,2,1,0:T(8,128)S(1)} %copy-done.5, f32[1,1,1,512,512]{4,3,2,1,0:T(8,128)} %copy-done.6, f32[2]{0:T(128)S(1)} %get-tuple-element.8, ...), kind=kOutput, calls=%fused_computation.25 | convolution fusion | flops 1077936128 | bytes 7864328 | tf_op jit(solution)/shard_map/xij,xjk->xik/dot_general | solution.py:41
  187.4 2.6 fusion.85
  190.1 3.0 fusion.8
  193.1 0.0 copy-start.3
  193.1 3.0 fusion.19
  196.1 0.0 copy-done.3
  196.1 2.0 fusion.86
  198.2 0.0 copy-start.2
  198.2 6.7 %fusion.5 = bf16[2,512,512]{2,1,0:T(8,128)(2,1)} fusion(f32[2,512,512]{2,1,0:T(8,128)} %fusion.86, f32[512,512]{1,0:T(8,128)S(1)} %get-tuple-element.10), kind=kOutput, calls=%fused_computation.16 | convolution fusion | flops 1074790400 | bytes 4194304 | tf_op jit(solution)/shard_map/xij,xjk->xik/dot_general | solution.py:41
  204.8 0.0 copy-done.2
  204.8 4.4 %fusion.24 = bf16[1,1,2,512,512]{4,3,2,1,0:T(8,128)(2,1)} fusion(bf16[2,512,512]{2,1,0:T(8,128)(2,1)} %fusion.19, f32[2,512,512]{2,1,0:T(8,128)S(1)} %copy-done.2, bf16[2,512,512]{2,1,0:T(8,128)(2,1)} %fusion.5, f32[2]{0:T(128)S(1)} %get-tuple-element.7, f32[512,512]{1,0:T(8,128)S(1)} %get-tuple-element.10), kind=kOutput, calls=%fused_computation.29 | convolution fusion | flops 1614282752 | bytes 6291464 | tf_op jit(solution)/shard_map/xij,xjk->xik/dot_general | solution.py:41
  209.2 3.0 convolution_convert_fusion
  212.2 0.0 all-gather.2.cloned.1.call-update
  212.3 88.8 %all-gather.2.cloned.1.call-done = bf16[4096,512]{1,0:T(8,128)(2,1)} async-done(((bf16[512,512]{1,0:T(8,128)(2,1)}), bf16[4096,512]{1,0:T(8,128)(2,1)}) %all-gather.2.cloned.1.call-update) | async-done | bytes 4194320 | tf_op jit(solution)/shard_map/all_gather | solution.py:106
  301.1 58.0 %all_to_all.47 = bf16[16,256,512]{2,1,0:T(8,128)(2,1)S(1)} all-to-all(bf16[16,256,512]{2,1,0:T(8,128)(2,1)} %bitcast.73), channel_id=1, replica_groups=mesh['rep'=8,'tp'=16] {'tp'}, dimensions={0} | all-to-all | bytes 8388608 | tf_op jit(solution)/shard_map/all_to_all | solution.py:107
  359.0 2.6 copy.24
  (1 shorter events, 0.0 us)
Async XLA Ops:
  117.7 33.2 %all-to-all-start.1 = ((bf16[8,1,256,512]{3,2,1,0:T(8,128)(2,1)}), bf16[8,1,256,512]{3,2,1,0:T(8,128)(2,1)}, u32[]{:S(2)}, u32[]{:S(2)}) async-start(bf16[8,1,256,512]{3,2,1,0:T(8,128)(2,1)} %get-tuple-element.5), calls=%async_computation.1 | async-start | bytes 4194304 | tf_op jit(solution)/shard_map/all_to_all | solution.py:36
  122.0 179.0 %all-gather.2.cloned.1.call-start = ((), (), s32[]{:S(2)}) async-start(), calls=%async_computation.4 | async-start | bytes 4718592 | tf_op jit(solution)/shard_map/all_gather | solution.py:106
  158.7 5.0 %copy-start.4 = (f32[1,1,1,512,512]{4,3,2,1,0:T(8,128)}, f32[1,1,1,512,512]{4,3,2,1,0:T(8,128)S(1)}, u32[]{:S(2)}) copy-start(f32[1,1,1,512,512]{4,3,2,1,0:T(8,128)S(1)} %convolution_bitcast_fusion) | copy-start | bytes 3145732
  158.7 5.0 %copy-start = (f32[512,512]{1,0:T(8,128)S(1)}, f32[512,512]{1,0:T(8,128)}, u32[]{:S(2)}) copy-start(f32[512,512]{1,0:T(8,128)} %get-tuple-element.9) | copy-start | bytes 3145732
  163.7 1.0 copy-start.6
  163.7 1.6 copy-start.1
  165.3 7.4 %copy-start.5 = (f32[1,1,1,512,512]{4,3,2,1,0:T(8,128)S(1)}, f32[1,1,1,512,512]{4,3,2,1,0:T(8,128)}, u32[]{:S(2)}) copy-start(f32[1,1,1,512,512]{4,3,2,1,0:T(8,128)} %copy-done.4) | copy-start | bytes 3145732
  193.1 3.0 copy-start.3
  198.2 6.7 %copy-start.2 = (f32[2,512,512]{2,1,0:T(8,128)S(1)}, f32[2,512,512]{2,1,0:T(8,128)}, u32[]{:S(2)}) copy-start(f32[2,512,512]{2,1,0:T(8,128)} %fusion.86) | copy-start | bytes 6291460
Sparse Core Ops, SparseCore 0:
  212.4 88.6 all-gather.1
where the time goes:
time: 369 us; the launch traced here: 368 us
  blocking collectives  147 us (40%)
  waiting for transfers between devices  116 us (31%)
  matrix products  56.4 us (15%)
  local copies, waits for them, and re-layouts  24.9 us (7%)
  between operations  14.1 us (4%)
  other arithmetic  5.79 us (2%)
  starting transfers between devices  4.39 us (1%)
    all_gather x1, waiting for transfers between devices, local(): gathered = lax.all_gather(to_strip(local_tiles), 'rep', axis=0, tiled=True)  88.8 us
    all_to_all x1, blocking collectives, local(): lax.all_to_all(picked, 'tp', split_axis=1, concat_axis=0, tiled=True)  59.7 us
    all_to_all x1, blocking collectives, local(): lax.all_to_all(gathered, 'tp', split_axis=0, concat_axis=1, tiled=True)  58 us
    dot_general x10, matrix products, multiply(): return jnp.einsum('xij,xjk->xik', left_side, right_side)  43.8 us
    all_to_all x1, blocking collectives, cut_exchange(): lax.all_to_all(share, axis, split_axis=0, concat_axis=0, tiled=True)  29.5 us
    all_to_all x1, waiting for transfers between devices, cut_exchange(): lax.all_to_all(share, axis, split_axis=0, concat_axis=0, tiled=True)  26.7 us
    unnamed x15, local copies, waits for them, and re-layouts  7.48 us
  transfers between devices with their start and end apart: 2, of which 2 were waited for; matrix products, arithmetic and copies ran while one was open for 1% of the time, Pallas kernels for 0%

commit v1 on v0

v1 whole, which is shorter than its diff:
```python
import jax
import jax.numpy as jnp
from jax import lax
from jax.sharding import Mesh, PartitionSpec as P

TILE = 512
NS_ITERS = 5
CORES = 2

damping = 0.001


def multiply(left_side, right_side):
    return jnp.einsum("xij,xjk->xik", left_side, right_side)


def inverse_roots(stat_stack):
    identity = jnp.eye(TILE, dtype=jnp.float32)
    frob_norm = jnp.sqrt(jnp.sum(stat_stack * stat_stack, axis=(1, 2), keepdims=True))
    current = stat_stack / frob_norm
    iterate = None
    for step in range(NS_ITERS):
        factor = (5.0 * identity - current) * 0.25
        iterate = factor if iterate is None else multiply(iterate, factor)
        if step + 1 < NS_ITERS:
            square = multiply(factor, factor)
            fourth = multiply(square, square)
            current = multiply(fourth, current)
    return (iterate * frob_norm ** (-0.25)).astype(jnp.bfloat16)


def local(deltas, staleness):
    replicas = lax.axis_size("rep")
    group = replicas * CORES
    picked = lax.dynamic_index_in_dim(deltas[0], staleness[0], 0, keepdims=False)
    rows = picked.shape[0]
    blocks = picked.reshape(rows, group, TILE).transpose(1, 0, 2)
    received = lax.all_to_all(blocks, ("rep", "core"), split_axis=0, concat_axis=0, tiled=True)
    tiles = received.reshape(replicas, TILE, TILE)
    left_gram = jnp.einsum("rik,rjk->ij", tiles, tiles, preferred_element_type=jnp.float32)
    right_gram = jnp.einsum("rki,rkj->ij", tiles, tiles, preferred_element_type=jnp.float32)
    mean_tile = (jnp.sum(tiles.astype(jnp.float32), axis=0) / replicas).astype(jnp.bfloat16)
    identity = jnp.eye(TILE, dtype=jnp.float32)
    stats = jnp.stack([left_gram, right_gram]) / (replicas * TILE) + damping * identity
    roots = inverse_roots(stats)
    half = jnp.dot(roots[0], mean_tile, preferred_element_type=jnp.float32).astype(jnp.bfloat16)
    tile = jnp.dot(half, roots[1], preferred_element_type=jnp.float32).astype(jnp.bfloat16)
    halves = tile.reshape(CORES, rows, TILE)
    outgoing = jnp.broadcast_to(halves[None], (replicas, CORES, rows, TILE)).reshape(group, rows, TILE)
    gathered = lax.all_to_all(outgoing, ("rep", "core"), split_axis=0, concat_axis=0, tiled=True)
    return gathered.transpose(1, 0, 2).reshape(rows, group * TILE)


def solution(mesh):
    shape = mesh.devices.shape
    split = Mesh(mesh.devices.reshape(shape[0], shape[1] // CORES, CORES), ("rep", "row", "core"))
    return jax.shard_map(
        local,
        mesh=split,
        in_specs=(P("rep", None, ("row", "core"), None), P("rep")),
        out_specs=P(("row", "core"), None),
        check_vma=False,
    )
```

time: 369 us -> 214 us (0.58)
  blocking collectives: 147 us -> 60.7 us
  waiting for transfers between devices: 116 us -> 52.9 us
  between operations: 14.1 us -> 0.76 us
  local copies, waits for them, and re-layouts: 24.9 us -> 31.6 us
    all_gather x1 -> x0, waiting for transfers between devices: 88.8 us -> none  [local(): gathered = lax.all_gather(to_strip(local_tiles), 'rep', axis=0, tiled=True)]
    all_to_all x3 -> x1, blocking collectives: 147 us -> 60.7 us  [local(): lax.all_to_all(outgoing, ('rep', 'core'), split_axis=0, concat_axis=0, ti...]
    all_to_all x1, waiting for transfers between devices: 26.7 us -> 52.9 us  [local(): lax.all_to_all(blocks, ('rep', 'core'), split_axis=0, concat_axis=0, tile...]
    reshape x0 -> x1, local copies, waits for them, and re-layouts: none -> 6.31 us  [local(): return gathered.transpose(1, 0, 2).reshape(rows, group * TILE)]
    all_to_all x2, local copies, waits for them, and re-layouts: 8.98 us -> 12.8 us  [the longest x1 6.43 us: local(): lax.all_to_all(outgoing, ('rep', 'core'), split_axis=0, concat_axis=0, ti...]
    split x1 -> x0, local copies, waits for them, and re-layouts: 3.81 us -> none  [cut_exchange(): jnp.split(blocks, cut_rows(blocks.shape[split_at], pieces), axis=split_at)]
    dot_general x10 -> x9, matrix products: 43.8 us -> 45.8 us  [multiply(): return jnp.einsum('xij,xjk->xik', left_side, right_side)]
    unnamed x15 -> x13, local copies, waits for them, and re-layouts: 7.48 us -> 7.42 us
  transfers between devices with their start and end apart: 2 -> 1, of which waited for: 2 -> 1; matrix products, arithmetic and copies ran while one was open for 1% -> 0% of each run, Pallas kernels for 0% -> 0%
where the time goes in v1:
time: 214 us; the launch traced here: 213 us
  blocking collectives  60.7 us (28%)
  matrix products  56 us (26%)
  waiting for transfers between devices  52.9 us (25%)
  local copies, waits for them, and re-layouts  31.6 us (15%)
  starting transfers between devices  7.33 us (3%)
  other arithmetic  3.63 us (2%)
    all_to_all x1, blocking collectives, local(): lax.all_to_all(outgoing, ('rep', 'core'), split_axis=0, concat_axis=0, ti...  60.7 us
    all_to_all x1, waiting for transfers between devices, local(): lax.all_to_all(blocks, ('rep', 'core'), split_axis=0, concat_axis=0, tile...  52.9 us
    dot_general x9, matrix products, multiply(): return jnp.einsum('xij,xjk->xik', left_side, right_side)  45.8 us
    unnamed x13, local copies, waits for them, and re-layouts  7.42 us
    all_to_all x1, starting transfers between devices, local(): lax.all_to_all(blocks, ('rep', 'core'), split_axis=0, concat_axis=0, tile...  7.33 us
    all_to_all x1, local copies, waits for them, and re-layouts, local(): lax.all_to_all(outgoing, ('rep', 'core'), split_axis=0, concat_axis=0, ti...  6.43 us
    all_to_all x1, local copies, waits for them, and re-layouts, local(): lax.all_to_all(blocks, ('rep', 'core'), split_axis=0, concat_axis=0, tile...  6.4 us
    reshape x1, local copies, waits for them, and re-layouts, local(): return gathered.transpose(1, 0, 2).reshape(rows, group * TILE)  6.31 us
  transfers between devices with their start and end apart: 1, of which 1 were waited for; matrix products, arithmetic and copies ran while one was open for 0% of the time, Pallas kernels for 0%

profile of v1, /device:TPU:1, one launch (start us, length us, event | category | flops | bytes accessed | tf_op | source)
XLA Modules:
  0.0 212.9 jit_solution(18375186076981674862)
XLA Ops:
  0.7 4.6 %constant_dynamic-slice_fusion = bf16[1,1,256,8192]{3,2,1,0:T(8,128)(2,1)} fusion(bf16[1,3,256,8192]{3,2,1,0:T(8,128)(2,1)} %param.2, s32[]{:T(128)S(6)} %select_n.4), kind=kLoop, calls=%fused_computation.49 | loop fusion | bytes 8388612 | tf_op jit(solution)/shard_map/jit(dynamic_index_in_dim)/dynamic_slice | solution.py:35
  5.3 6.4 %copy.18 = bf16[1,1,256,8192]{2,3,1,0:T(8,128)(2,1)} copy(bf16[1,1,256,8192]{3,2,1,0:T(8,128)(2,1)} %constant_dynamic-slice_fusion) | data formatting | bytes 8388608
  11.7 7.3 %all-to-all-start = ((bf16[16,256,512]{1,2,0:T(8,128)(2,1)}), bf16[16,256,512]{1,2,0:T(8,128)(2,1)}, u32[]{:S(2)}, u32[]{:S(2)}) async-start(bf16[16,256,512]{1,2,0:T(8,128)(2,1)} %bitcast.43), calls=%async_computation | async-start | bytes 8388608 | tf_op jit(solution)/shard_map/all_to_all | solution.py:38
  19.0 0.1 fusion.49
  19.2 0.0 copy-start.4
  19.2 0.1 fusion.48
  19.3 52.9 %all-to-all-done = bf16[16,256,512]{1,2,0:T(8,128)(2,1)} async-done(((bf16[16,256,512]{1,2,0:T(8,128)(2,1)}), bf16[16,256,512]{1,2,0:T(8,128)(2,1)}, u32[]{:S(2)}, u32[]{:S(2)}) %all-to-all-start) | async-done | bytes 4194336 | tf_op jit(solution)/shard_map/all_to_all | solution.py:38
  72.1 6.4 %copy.13 = bf16[16,256,512]{2,1,0:T(8,128)(2,1)} copy(bf16[16,256,512]{1,2,0:T(8,128)(2,1)} %all-to-all-done) | data formatting | bytes 8388608 | tf_op jit(solution)/shard_map/all_to_all | solution.py:38
  78.5 0.0 copy-start
  78.6 5.9 %convolution_bitcast_fusion = f32[1,512,512]{2,1,0:T(8,128)S(1)} fusion(bf16[8,512,512]{2,1,0:T(8,128)(2,1)} %bitcast.40), kind=kOutput, calls=%fused_computation.24 | convolution fusion | flops 2147483648 | bytes 5242880 | tf_op jit(solution)/shard_map/rki,rkj->ij/dot_general | solution.py:41
  84.5 0.0 copy-done
  84.5 0.0 copy-start.1
  84.5 2.4 %convolution_bitcast_fusion.1 = f32[1,512,512]{2,1,0:T(8,128)S(1)} fusion(bf16[8,512,512]{2,1,0:T(8,128)(2,1)S(1)} %bitcast.42), kind=kOutput, calls=%fused_computation.25 | convolution fusion | flops 2147483648 | bytes 5242880 | tf_op jit(solution)/shard_map/rik,rjk->ij/dot_general | solution.py:40
  86.9 0.0 copy-start.5
  86.9 1.0 copy-done.5
  87.9 0.5 multiply_reduce_fusion
  88.4 6.2 %fusion.13 = bf16[2,512,512]{2,1,0:T(8,128)(2,1)} fusion(f32[512,512]{1,0:T(8,128)S(1)} %fusion.49, f32[1,512,512]{2,1,0:T(8,128)S(1)} %convolution_bitcast_fusion, f32[1,512,512]{2,1,0:T(8,128)} %copy-done.5, f32[2]{0:T(128)S(1)} %get-tuple-element.6, f32[512,512]{1,0:T(8,128)S(1)} %fusion.48), kind=kOutput, calls=%fused_computation.18 | convolution fusion | flops 1076887552 | bytes 5242888 | tf_op jit(solution)/shard_map/xij,xjk->xik/dot_general | solution.py:14
  94.5 0.0 copy-done.1
  94.5 3.7 %fusion.68 = f32[2,512,512]{2,1,0:T(8,128)} fusion(bf16[2,512,512]{2,1,0:T(8,128)(2,1)} %fusion.13, f32[1,512,512]{2,1,0:T(8,128)S(1)} %convolution_bitcast_fusion, f32[1,512,512]{2,1,0:T(8,128)} %copy-done.5, f32[2]{0:T(128)S(1)} %get-tuple-element.6, f32[512,512]{1,0:T(8,128)S(1)} %fusion.48), kind=kOutput, calls=%fused_computation.57 | convolution fusion | flops 538968064 | bytes 6291464 | tf_op jit(solution)/shard_map/xij,xjk->xik/dot_general | solution.py:14
  98.2 0.0 copy-done.4
  98.2 6.4 %fusion.10 = bf16[2,512,512]{2,1,0:T(8,128)(2,1)} fusion(f32[2,512,512]{2,1,0:T(8,128)} %fusion.68, f32[512,512]{1,0:T(8,128)S(1)} %fusion.49), kind=kOutput, calls=%fused_computation.16 | convolution fusion | flops 1074790400 | bytes 4194304 | tf_op jit(solution)/shard_map/xij,xjk->xik/dot_general | solution.py:14
  104.6 2.6 %fusion.72 = f32[2,512,512]{2,1,0:T(8,128)S(1)} fusion(bf16[2,512,512]{2,1,0:T(8,128)(2,1)} %fusion.10, f32[2,512,512]{2,1,0:T(8,128)} %fusion.68), kind=kOutput, calls=%fused_computation.58 | convolution fusion | flops 536870912 | bytes 5242880 | tf_op jit(solution)/shard_map/xij,xjk->xik/dot_general | solution.py:14
  107.3 5.7 %fusion.17 = bf16[2,512,512]{2,1,0:T(8,128)(2,1)} fusion(f32[2,512,512]{2,1,0:T(8,128)S(1)} %fusion.72, f32[2,512,512]{2,1,0:T(8,128)} %fusion.68, f32[512,512]{1,0:T(8,128)} %copy-done.4, f32[1,512,512]{2,1,0:T(8,128)} %copy-done.1, f32[1,512,512]{2,1,0:T(8,128)} %copy-done.5, f32[2]{0:T(128)S(1)} %get-tuple-element.6, f32[512,512]{1,0:T(8,128)S(1)} %fusion.48), kind=kOutput, calls=%fused_computation.21 | convolution fusion | flops 1078984704 | bytes 9437192 | tf_op jit(solution)/shard_map/xij,xjk->xik/dot_general | solution.py:14
  113.0 5.7 %fusion.7 = bf16[2,512,512]{2,1,0:T(8,128)(2,1)} fusion(f32[2,512,512]{2,1,0:T(8,128)S(1)} %fusion.72, f32[512,512]{1,0:T(8,128)} %copy-done.4), kind=kOutput, calls=%fused_computation.14 | convolution fusion | flops 1074790400 | bytes 4194304 | tf_op jit(solution)/shard_map/xij,xjk->xik/dot_general | solution.py:14
  118.7 0.0 copy-start.3
  118.7 3.0 %convert_reduce_fusion = f32[512,512]{1,0:T(8,128)S(1)} fusion(bf16[8,512,512]{2,1,0:T(8,128)(2,1)} %bitcast.41), kind=kLoop, calls=%fused_computation | loop fusion | flops 3932160 | bytes 5242880 | tf_op jit(solution)/shard_map/reduce_sum | solution.py:42
  121.7 0.0 copy-done.3
  121.7 2.2 %fusion.73 = f32[2,512,512]{2,1,0:T(8,128)} fusion(bf16[2,512,512]{2,1,0:T(8,128)(2,1)S(1)} %copy-done.3, f32[2,512,512]{2,1,0:T(8,128)S(1)} %fusion.72), kind=kOutput, calls=%fused_computation.59 | convolution fusion | flops 536870912 | bytes 5242880 | tf_op jit(solution)/shard_map/xij,xjk->xik/dot_general | solution.py:14
  123.9 0.0 copy-start.2
  123.9 8.2 %fusion.4 = bf16[2,512,512]{2,1,0:T(8,128)(2,1)} fusion(f32[2,512,512]{2,1,0:T(8,128)} %fusion.73, f32[512,512]{1,0:T(8,128)} %copy-done.4), kind=kOutput, calls=%fused_computation.12 | convolution fusion | flops 1074790400 | bytes 4194304 | tf_op jit(solution)/shard_map/xij,xjk->xik/dot_general | solution.py:14
  132.1 0.0 copy-done.2
  132.1 5.1 %multiply_convert_fusion = bf16[2,512,512]{2,1,0:T(8,128)(2,1)} fusion(bf16[2,512,512]{2,1,0:T(8,128)(2,1)} %fusion.17, f32[2,512,512]{2,1,0:T(8,128)S(1)} %copy-done.2, bf16[2,512,512]{2,1,0:T(8,128)(2,1)} %fusion.4, f32[2]{0:T(128)S(1)} %get-tuple-element.5, f32[512,512]{1,0:T(8,128)} %copy-done.4), kind=kOutput, calls=%fused_computation.3 | convolution fusion | flops 1614282752 | bytes 6291464 | tf_op jit(solution)/shard_map/xij,xjk->xik/dot_general | solution.py:14
  137.1 1.9 convolution_convert_fusion
  139.1 0.4 broadcast_in_dim.5
  139.5 60.7 %all_to_all.10 = bf16[16,256,512]{2,1,0:T(8,128)(2,1)} all-to-all(bf16[16,256,512]{2,1,0:T(8,128)(2,1)S(1)} %bitcast.44), channel_id=1, replica_groups=mesh['rep'=8,'row'=8,'core'=2] {'rep','core'}, dimensions={0} | all-to-all | bytes 8388608 | tf_op jit(solution)/shard_map/all_to_all | solution.py:50
  200.2 6.4 %copy.15 = bf16[16,256,512]{1,2,0:T(8,128)(2,1)} copy(bf16[16,256,512]{2,1,0:T(8,128)(2,1)} %all_to_all.10) | data formatting | bytes 8388608 | tf_op jit(solution)/shard_map/all_to_all | solution.py:50
  206.6 6.3 %copy.16 = bf16[256,8192]{1,0:T(8,128)(2,1)} copy(bf16[256,8192]{0,1:T(8,128)(2,1)} %bitcast.45) | data formatting | bytes 8388608 | tf_op jit(solution)/shard_map/reshape | solution.py:51
  (1 shorter events, 0.0 us)
Async XLA Ops:
  11.7 60.4 %all-to-all-start = ((bf16[16,256,512]{1,2,0:T(8,128)(2,1)}), bf16[16,256,512]{1,2,0:T(8,128)(2,1)}, u32[]{:S(2)}, u32[]{:S(2)}) async-start(bf16[16,256,512]{1,2,0:T(8,128)(2,1)} %bitcast.43), calls=%async_computation | async-start | bytes 8388608 | tf_op jit(solution)/shard_map/all_to_all | solution.py:38
  19.2 79.0 %copy-start.4 = (f32[512,512]{1,0:T(8,128)}, f32[512,512]{1,0:T(8,128)S(1)}, u32[]{:S(2)}) copy-start(f32[512,512]{1,0:T(8,128)S(1)} %fusion.49) | copy-start | bytes 3145732
  78.5 6.0 %copy-start = (bf16[16,256,512]{2,1,0:T(8,128)(2,1)S(1)}, bf16[16,256,512]{2,1,0:T(8,128)(2,1)}, u32[]{:S(2)}) copy-start(bf16[16,256,512]{2,1,0:T(8,128)(2,1)} %copy.13) | copy-start | bytes 12582916
  84.5 10.0 %copy-start.1 = (f32[1,512,512]{2,1,0:T(8,128)}, f32[1,512,512]{2,1,0:T(8,128)S(1)}, u32[]{:S(2)}) copy-start(f32[1,512,512]{2,1,0:T(8,128)S(1)} %convolution_bitcast_fusion) | copy-start | bytes 3145732
  86.9 1.0 copy-start.5
  118.7 3.0 %copy-start.3 = (bf16[2,512,512]{2,1,0:T(8,128)(2,1)S(1)}, bf16[2,512,512]{2,1,0:T(8,128)(2,1)}, u32[]{:S(2)}) copy-start(bf16[2,512,512]{2,1,0:T(8,128)(2,1)} %fusion.7) | copy-start | bytes 3145732
  123.9 8.2 %copy-start.2 = (f32[2,512,512]{2,1,0:T(8,128)S(1)}, f32[2,512,512]{2,1,0:T(8,128)}, u32[]{:S(2)}) copy-start(f32[2,512,512]{2,1,0:T(8,128)} %fusion.73) | copy-start | bytes 6291460
